TPU v7x, 256 devices: a whole 4x4x8 slice. The times are simulated.
256 devices in a mesh: kx: 16 (over z, x_lo), ky: 4 (over x_hi, core), kz: 4 (over y).
Axes of the slice: x: 4 (x_hi: 2, x_lo: 2; x = x_hi * 2 + x_lo), y: 4, z: 8, core: 2. Of those that a mesh axis runs over, the one named last changes fastest.
Arguments:
- coefficients: bfloat16 [2, 16, 4, 4, 512, 2048], P(None, 'kx', 'ky', 'kz'), may hold values from -1 to 1
- shift_blocks: int32 [3], replicated, may hold values from 1 to 15, as said below
Outputs:
- centre: float32 [3, 512], replicated
- spread: float32 [3, 512], replicated
- coherence: float32 [3, 16, 4, 4], P(None, 'kx', 'ky', 'kz')
Inputs may be any that keep to these rules, and one draw needn't show every extreme that they name: The coefficients one period further along direction d are those of the first k-point of the string with plane-wave index g read at (g + 128 * shift_blocks[d]) mod 2048.
All inputs are finite; a program needn't handle non-finite values.
Results may differ from a plain program's by a relative error of at most 0.0003.
Values may be sent and summed in bfloat16 or wider, within the bound.
A program may use at most 128 MiB of HBM per device.

v0:
```python
import jax
import jax.numpy as jnp
from jax import lax
from jax.sharding import Mesh
from jax.sharding import PartitionSpec as P

KX = ("kx_0", "kx_1")
KY = ("ky_0", "ky_1")
KX_KY_KZ = ("kx_0", "kx_1", "ky_0", "ky_1", "kz")


def passed_along(value, axis, steps):
    count = lax.axis_size(axis)
    pairs = [(source, (source + steps) % count) for source in range(count)]
    return lax.ppermute(value, axis, pairs)


def one_axis_at_a_time(array, axes):
    for axis in axes:
        array = lax.psum(array, axis)
    return array


def pair_measure(own_point, partner):
    bands = own_point.shape[1]
    left_side = jnp.concatenate([own_point[0], own_point[1]], axis=1)
    right_side = jnp.concatenate(
        [
            jnp.concatenate([partner[0], partner[1]], axis=1),
            jnp.concatenate([partner[1], -partner[0]], axis=1),
        ],
        axis=0,
    )
    product = lax.dot_general(
        left_side, right_side, (((1,), (1,)), ((), ())), preferred_element_type=jnp.float32
    )
    real_part = product[:, :bands]
    imag_part = product[:, bands:]
    phases = jnp.arctan2(jnp.diagonal(imag_part), jnp.diagonal(real_part))
    coherence = jnp.sum(real_part * real_part + imag_part * imag_part) / bands
    return (phases, coherence)


def shards(coefficients, shift_blocks):
    planes = coefficients.shape[1]
    bands = coefficients.shape[4]
    width = coefficients.shape[5]
    own_planes = coefficients.reshape(2, planes, bands, width)
    shifts = shift_blocks * 128
    measure = jax.vmap(pair_measure, in_axes=(1, 1))
    next_first = passed_along(own_planes[:, 0], KX, -1)
    x_wrap = lax.axis_index(KX) == lax.axis_size(KX) - 1
    next_first = jnp.where(x_wrap, jnp.roll(next_first, -shifts[0], axis=-1), next_first)
    x_partner = jnp.concatenate([own_planes[:, 1:], next_first[:, None]], axis=1)
    x_phases, x_coherence = measure(own_planes, x_partner)
    earlier = passed_along(own_planes, KY, 1)
    y_wrap = lax.axis_index(KY) == 0
    y_partner = jnp.where(y_wrap, jnp.roll(own_planes, -shifts[1], axis=-1), own_planes)
    y_phases, y_earlier = measure(earlier, y_partner)
    y_coherence = passed_along(y_earlier, KY, -1)
    z_later = passed_along(own_planes, "kz", -1)
    z_wrap = lax.axis_index("kz") == lax.axis_size("kz") - 1
    z_partner = jnp.where(z_wrap, jnp.roll(z_later, -shifts[2], axis=-1), z_later)
    z_phases, z_coherence = measure(own_planes, z_partner)
    phases = jnp.stack([x_phases, y_phases, z_phases])
    coherence = jnp.stack([x_coherence, y_coherence, z_coherence]).reshape(3, planes, 1, 1)
    k_total = planes * lax.axis_size(KX) * lax.axis_size(KY) * lax.axis_size("kz")
    counts = jnp.array(
        [planes * lax.axis_size(KX), lax.axis_size(KY), lax.axis_size("kz")], jnp.float32
    )
    phase_sum = jnp.sum(phases, axis=1)
    totals, squares = (
        one_axis_at_a_time(phase_sum, KX_KY_KZ),
        one_axis_at_a_time(jnp.sum(phases * phases, axis=1), KX_KY_KZ),
    )
    mean_phase = totals / k_total
    variance = squares / k_total - mean_phase * mean_phase
    centre = -counts[:, None] * mean_phase / (2.0 * jnp.pi)
    spread = (counts[:, None] / (2.0 * jnp.pi)) ** 2 * variance
    return (centre, spread, coherence)


def solution(mesh):
    split = Mesh(
        mesh.devices.reshape(8, 2, 2, 2, mesh.shape["kz"]), ("kx_0", "kx_1", "ky_0", "ky_1", "kz")
    )
    in_specs = (P(None, KX, KY, "kz", None, None), P())
    out_specs = (P(), P(), P(None, KX, KY, "kz"))
    return jax.shard_map(
        shards, mesh=split, in_specs=in_specs, out_specs=out_specs, check_vma=False
    )
```

profile of v0, /device:TPU:2, one launch (start us, length us, event | category | flops | bytes accessed | tf_op | source)
XLA Modules:
  0.0 270.2 jit_solution(11188901696247821564)
XLA Ops:
  0.6 3.1 %collective-permute-start.2 = (bf16[2,1,512,2048]{3,2,0,1:T(8,128)(2,1)}, bf16[2,1,512,2048]{3,2,0,1:T(8,128)(2,1)}, u32[]{:S(2)}, u32[]{:S(2)}) collective-permute-start(bf16[2,1,512,2048]{3,2,0,1:T(8,128)(2,1)} %bitcast.97), channel_id=1, source_target_pairs={{0,3},{1,0},{2,1},{3,2},{4,7},{5,4},{6,5},{7,6},{8,11},{9,8},{10,9... | collective-permute-start | bytes 12582920 | tf_op jit(solution)/shard_map/ppermute | solution.py:15
  8.2 6.5 %fusion.39 = bf16[2,1,512,2048]{3,2,1,0:T(8,128)(2,1)S(1)} fusion(bf16[2,1,512,2048]{3,2,0,1:T(8,128)(2,1)} %bitcast.100, s32[]{:T(128)S(6)} %select_n.67, pred[]{:T(512)S(6)} %eq.14), kind=kLoop, calls=%fused_computation.81 | loop fusion | flops 10485760 | bytes 8388613 | tf_op jit(solution)/shard_map/jit(_where)/select_n | solution.py:58
  18.3 4.2 %fusion.24 = bf16[2,1,512,2048]{3,2,0,1:T(8,128)(2,1)S(1)} fusion(bf16[2,1,512,2048]{3,2,0,1:T(8,128)(2,1)S(1)} %bitcast.101, s32[]{:T(128)S(6)} %select_n.67, pred[]{:T(512)S(6)} %eq.14), kind=kLoop, calls=%fused_computation.39 | loop fusion | flops 10485760 | bytes 8388613 | tf_op jit(solution)/shard_map/jit(_where)/select_n | solution.py:58
  26.5 67.3 %collective-permute-done.2 = bf16[2,1,512,2048]{3,2,0,1:T(8,128)(2,1)} collective-permute-done((bf16[2,1,512,2048]{3,2,0,1:T(8,128)(2,1)}, bf16[2,1,512,2048]{3,2,0,1:T(8,128)(2,1)}, u32[]{:S(2)}, u32[]{:S(2)}) %collective-permute-start.2) | collective-permute-done | bytes 4194336 | tf_op jit(solution)/shard_map/ppermute | solution.py:15
  93.9 7.8 %fusion.40 = bf16[2,1,512,2048]{3,2,1,0:T(8,128)(2,1)S(1)} fusion(bf16[2,1,512,2048]{3,2,0,1:T(8,128)(2,1)} %collective-permute-done.2, s32[]{:T(128)S(6)} %select_n.69, pred[]{:T(512)S(6)} %eq.15), kind=kLoop, calls=%fused_computation.82 | loop fusion | flops 10485760 | bytes 8388613 | tf_op jit(solution)/shard_map/jit(_where)/select_n | solution.py:63
  102.0 8.0 %fusion.22 = bf16[2,1,512,2048]{3,2,0,1:T(8,128)(2,1)S(1)} fusion(bf16[2,1,512,2048]{3,2,0,1:T(8,128)(2,1)} %collective-permute-done.2, s32[]{:T(128)S(6)} %select_n.69, pred[]{:T(512)S(6)} %eq.15), kind=kLoop, calls=%fused_computation.37 | loop fusion | flops 10485760 | bytes 8388613 | tf_op jit(solution)/shard_map/jit(_where)/select_n | solution.py:63
  110.1 8.2 %fusion.29 = f32[1,512,1024]{2,1,0:T(8,128)} fusion(bf16[1,512,2048]{2,1,0:T(8,128)(2,1)S(1)} %fusion.36, bf16[1,512,2048]{2,1,0:T(8,128)(2,1)S(1)} %slice_bitcast_fusion, bf16[1,512,2048]{2,1,0:T(8,128)(2,1)S(1)} %slice_bitcast_fusion.1, bf16[1,512,2048]{2,1,0:T(8,128)(2,1)} %get-tuple-element.18, bf16[1,512,2048]{2,1,0:T(8,128)(2,1)} %get-tuple-element.17), kind=kOutput, calls=%fused_computation.54 | convolution fusion | flops 4336910336 | bytes 12582912 | tf_op jit(solution)/shard_map/vmap()/dot_general | solution.py:34
  120.8 4.5 %gather_fusion.4 = f32[512]{0:T(512)S(1)} fusion(f32[512,512]{1,0:T(8,128)S(1)} %get-tuple-element.27, s32[512]{0:T(512)S(1)} %bitcast.91), kind=kCustom, calls=%fused_computation.4 | custom fusion | bytes 8192 | tf_op jit(solution)/shard_map/vmap(jit(diagonal))/cond/branch_0_fun/gather | solution.py:39
  125.3 4.5 %gather_fusion.5 = f32[512]{0:T(512)S(1)} fusion(f32[512,512]{1,0:T(8,128)S(1)} %get-tuple-element.26, s32[512]{0:T(512)S(1)} %bitcast.92), kind=kCustom, calls=%fused_computation.5 | custom fusion | bytes 8192 | tf_op jit(solution)/shard_map/vmap(jit(diagonal))/cond/branch_0_fun/gather | solution.py:39
  129.9 3.3 %slice_bitcast_fusion.5 = bf16[1,512,2048]{2,1,0:T(8,128)(2,1)} fusion(bf16[2,1,512,2048]{3,2,1,0:T(8,128)(2,1)} %bitcast.12), kind=kLoop, calls=%fused_computation.51 | loop fusion | bytes 4194304 | tf_op jit(solution)/shard_map/vmap()/squeeze;vmap()/transpose | solution.py:26
  133.2 3.2 %slice_bitcast_fusion.4 = bf16[1,512,2048]{2,1,0:T(8,128)(2,1)} fusion(bf16[2,1,512,2048]{3,2,0,1:T(8,128)(2,1)} %collective-permute-done.1), kind=kLoop, calls=%fused_computation.50 | loop fusion | bytes 4194304 | tf_op jit(solution)/shard_map/vmap()/squeeze;vmap()/transpose | solution.py:26
  136.4 8.1 %fusion.30 = f32[1,512,1024]{2,1,0:T(8,128)} fusion(bf16[1,512,2048]{2,1,0:T(8,128)(2,1)S(1)} %copy-done.1, bf16[1,512,2048]{2,1,0:T(8,128)(2,1)S(1)} %copy-done.3, bf16[1,512,2048]{2,1,0:T(8,128)(2,1)S(1)} %copy-done.2, bf16[1,512,2048]{2,1,0:T(8,128)(2,1)} %slice_bitcast_fusion.4, bf16[1,512,2048]{2,1,0:T(8,128)(2,1)} %slice_bitcast_fusion.5), kind=kOutput, calls=%fused_computation.55 | convolution fusion | flops 4336910336 | bytes 12582912 | tf_op jit(solution)/shard_map/vmap()/dot_general | solution.py:34
  147.0 4.5 %gather_fusion.2 = f32[512]{0:T(512)S(1)} fusion(f32[512,512]{1,0:T(8,128)S(1)} %get-tuple-element.24, s32[512]{0:T(512)S(1)} %bitcast.93), kind=kCustom, calls=%fused_computation.2 | custom fusion | bytes 8192 | tf_op jit(solution)/shard_map/vmap(jit(diagonal))/cond/branch_0_fun/gather | solution.py:39
  151.5 4.5 %gather_fusion.3 = f32[512]{0:T(512)S(1)} fusion(f32[512,512]{1,0:T(8,128)S(1)} %get-tuple-element.23, s32[512]{0:T(512)S(1)} %bitcast.94), kind=kCustom, calls=%fused_computation.3 | custom fusion | bytes 8192 | tf_op jit(solution)/shard_map/vmap(jit(diagonal))/cond/branch_0_fun/gather | solution.py:39
  156.1 6.7 %fusion.26 = bf16[2,512,2048]{2,1,0:T(8,128)(2,1)S(1)} fusion(bf16[2,512,2048]{2,1,0:T(8,128)(2,1)} %collective-permute-done, s32[]{:T(128)S(6)} %select_n.58, pred[]{:T(512)S(6)} %eq.13), kind=kLoop, calls=%fused_computation.41 | loop fusion | flops 10485760 | bytes 8388613 | tf_op jit(solution)/shard_map/jit(_where)/select_n | solution.py:53
  163.2 8.1 %fusion.31 = f32[1,512,1024]{2,1,0:T(8,128)} fusion(bf16[1,512,2048]{2,1,0:T(8,128)(2,1)S(1)} %get-tuple-element.15, bf16[1,512,2048]{2,1,0:T(8,128)(2,1)S(1)} %get-tuple-element.16, bf16[1,512,2048]{2,1,0:T(8,128)(2,1)S(1)} %get-tuple-element.14, bf16[1,512,2048]{2,1,0:T(8,128)(2,1)} %get-tuple-element.18, bf16[1,512,2048]{2,1,0:T(8,128)(2,1)} %get-tuple-element.17), kind=kOutput, calls=%fused_computation.56 | convolution fusion | flops 4336910336 | bytes 12582912 | tf_op jit(solution)/shard_map/vmap()/dot_general | solution.py:34
  171.3 2.5 add_reduce_fusion.2
  173.8 4.5 %gather_fusion = f32[512]{0:T(512)S(1)} fusion(f32[512,512]{1,0:T(8,128)S(1)} %get-tuple-element.21, s32[512]{0:T(512)S(1)} %bitcast.95), kind=kCustom, calls=%fused_computation | custom fusion | bytes 8192 | tf_op jit(solution)/shard_map/vmap(jit(diagonal))/cond/branch_0_fun/gather | solution.py:39
  178.4 4.5 %gather_fusion.1 = f32[512]{0:T(512)S(1)} fusion(f32[512,512]{1,0:T(8,128)S(1)} %get-tuple-element.20, s32[512]{0:T(512)S(1)} %bitcast.96), kind=kCustom, calls=%fused_computation.1 | custom fusion | bytes 8192 | tf_op jit(solution)/shard_map/vmap(jit(diagonal))/cond/branch_0_fun/gather | solution.py:39
  187.1 32.8 %all-reduce = (f32[3,512]{1,0:T(4,128)S(1)}, f32[3,512]{1,0:T(4,128)S(1)}) all-reduce(f32[3,512]{1,0:T(4,128)S(1)} %maximum_bitcast_fusion.23, f32[3,512]{1,0:T(4,128)S(1)} %maximum_multiply_fusion), channel_id=1, replica_groups=mesh['kx_0'=8,'kx_1'=2,'ky_0'=2,'ky_1'=2,'kz'=4] {'kx_0'}, use_global_device_ids=true, to_apply=%region_0.2 | all-reduce | flops 3072 | bytes 24576 | tf_op jit(solution)/shard_map/psum | solution.py:20
  219.8 19.9 %all-reduce.4 = (f32[3,512]{1,0:T(4,128)S(1)}, f32[3,512]{1,0:T(4,128)S(1)}) all-reduce(f32[3,512]{1,0:T(4,128)S(1)} %get-tuple-element.4, f32[3,512]{1,0:T(4,128)S(1)} %get-tuple-element.5), channel_id=1, replica_groups=mesh['kx_0'=8,'kx_1'=2,'ky_0'=2,'ky_1'=2,'kz'=4] {'kx_1'}, use_global_device_ids=true, to_apply=%region_1.3 | all-reduce | flops 3072 | bytes 24576 | tf_op jit(solution)/shard_map/psum | solution.py:20
  239.7 10.5 %all-reduce.3 = (f32[3,512]{1,0:T(4,128)S(1)}, f32[3,512]{1,0:T(4,128)S(1)}) all-reduce(f32[3,512]{1,0:T(4,128)S(1)} %get-tuple-element.12, f32[3,512]{1,0:T(4,128)S(1)} %get-tuple-element.13), channel_id=1, replica_groups=mesh['kx_0'=8,'kx_1'=2,'ky_0'=2,'ky_1'=2,'kz'=4] {'ky_0'}, use_global_device_ids=true, to_apply=%region_2.4 | all-reduce | flops 3072 | bytes 24576 | tf_op jit(solution)/shard_map/psum | solution.py:20
  250.2 3.3 %all-reduce.2 = (f32[3,512]{1,0:T(4,128)S(1)}, f32[3,512]{1,0:T(4,128)S(1)}) all-reduce(f32[3,512]{1,0:T(4,128)S(1)} %get-tuple-element.10, f32[3,512]{1,0:T(4,128)S(1)} %get-tuple-element.11), channel_id=1, replica_groups=mesh['kx_0'=8,'kx_1'=2,'ky_0'=2,'ky_1'=2,'kz'=4] {'ky_1'}, use_global_device_ids=true, to_apply=%region_3.5 | all-reduce | flops 3072 | bytes 24576 | tf_op jit(solution)/shard_map/psum | solution.py:20
  253.5 14.9 %all-reduce.1 = (f32[3,512]{1,0:T(4,128)S(1)}, f32[3,512]{1,0:T(4,128)S(1)}) all-reduce(f32[3,512]{1,0:T(4,128)S(1)} %get-tuple-element.8, f32[3,512]{1,0:T(4,128)S(1)} %get-tuple-element.9), channel_id=1, replica_groups=mesh['kx_0'=8,'kx_1'=2,'ky_0'=2,'ky_1'=2,'kz'=4] {'kz'}, use_global_device_ids=true, to_apply=%region_4.6 | all-reduce | flops 3072 | bytes 24576 | tf_op jit(solution)/shard_map/psum | solution.py:20
  (38 shorter events, 19.3 us)
Async XLA Ops:
  0.6 93.2 %collective-permute-start.2 = (bf16[2,1,512,2048]{3,2,0,1:T(8,128)(2,1)}, bf16[2,1,512,2048]{3,2,0,1:T(8,128)(2,1)}, u32[]{:S(2)}, u32[]{:S(2)}) collective-permute-start(bf16[2,1,512,2048]{3,2,0,1:T(8,128)(2,1)} %bitcast.97), channel_id=1, source_target_pairs={{0,3},{1,0},{2,1},{3,2},{4,7},{5,4},{6,5},{7,6},{8,11},{9,8},{10,9... | collective-permute-start | bytes 12582920 | tf_op jit(solution)/shard_map/ppermute | solution.py:15
  3.7 126.1 %collective-permute-start.1 = (bf16[2,1,512,2048]{3,2,0,1:T(8,128)(2,1)}, bf16[2,1,512,2048]{3,2,0,1:T(8,128)(2,1)}, u32[]{:S(2)}, u32[]{:S(2)}) collective-permute-start(bf16[2,1,512,2048]{3,2,0,1:T(8,128)(2,1)} %bitcast.98), channel_id=1, source_target_pairs={{0,4},{4,8},{8,12},{12,0},{1,5},{5,9},{9,13},{13,1},{2,6},{6,10},{... | collective-permute-start | bytes 12582920 | tf_op jit(solution)/shard_map/ppermute | solution.py:15
  3.7 152.3 %collective-permute-start = (bf16[2,512,2048]{2,1,0:T(8,128)(2,1)}, bf16[2,512,2048]{2,1,0:T(8,128)(2,1)}, u32[]{:S(2)}, u32[]{:S(2)}) collective-permute-start(bf16[2,512,2048]{2,1,0:T(8,128)(2,1)} %bitcast.99), channel_id=1, source_target_pairs={{0,240},{16,0},{32,16},{48,32},{64,48},{80,64},{96,80},{112,96},{1... | collective-permute-start | bytes 12582920 | tf_op jit(solution)/shard_map/ppermute | solution.py:15
  14.7 3.6 %copy-start = (bf16[2,1,1,1,512,2048]{5,4,3,2,1,0:T(8,128)(2,1)S(1)}, bf16[2,1,1,1,512,2048]{5,4,3,2,1,0:T(8,128)(2,1)}, u32[]{:S(2)}) copy-start(bf16[2,1,1,1,512,2048]{5,4,3,2,1,0:T(8,128)(2,1)} %param.5) | copy-start | bytes 12582916
  129.9 6.6 %copy-start.1 = (bf16[1,512,2048]{2,1,0:T(8,128)(2,1)S(1)}, bf16[1,512,2048]{2,1,0:T(8,128)(2,1)}, u32[]{:S(2)}) copy-start(bf16[1,512,2048]{2,1,0:T(8,128)(2,1)} %fusion.35) | copy-start | bytes 6291460
  129.9 6.5 %copy-start.2 = (bf16[1,512,2048]{2,1,0:T(8,128)(2,1)S(1)}, bf16[1,512,2048]{2,1,0:T(8,128)(2,1)}, u32[]{:S(2)}) copy-start(bf16[1,512,2048]{2,1,0:T(8,128)(2,1)} %slice_bitcast_fusion.3) | copy-start | bytes 6291460
  129.9 6.5 %copy-start.3 = (bf16[1,512,2048]{2,1,0:T(8,128)(2,1)S(1)}, bf16[1,512,2048]{2,1,0:T(8,128)(2,1)}, u32[]{:S(2)}) copy-start(bf16[1,512,2048]{2,1,0:T(8,128)(2,1)} %slice_bitcast_fusion.2) | copy-start | bytes 6291460
  171.3 97.1 %copy-start.4 = (f32[3]{0:T(128)S(1)}, f32[3]{0:T(128)}, u32[]{:S(2)}) copy-start(f32[3]{0:T(128)} %constant.109) | copy-start | bytes 40
  171.3 97.1 %copy-start.5 = (f32[3]{0:T(128)S(1)}, f32[3]{0:T(128)}, u32[]{:S(2)}) copy-start(f32[3]{0:T(128)} %constant.106) | copy-start | bytes 40
  184.2 84.9 %collective-permute-start.3 = (f32[1]{0:T(128)}, f32[1]{0:T(128)}, u32[]{:S(2)}, u32[]{:S(2)}) collective-permute-start(f32[1]{0:T(128)} %bitcast.39), channel_id=1, source_target_pairs={{0,12},{4,0},{8,4},{12,8},{1,13},{5,1},{9,5},{13,9},{2,14},{6,2},{... | collective-permute-start | bytes 20 | tf_op jit(solution)/shard_map/ppermute | solution.py:15
where the time goes:
time: 271 us; the launch traced here: 270 us
  blocking collectives  81.3 us (30%)
  waiting for transfers between devices  67.3 us (25%)
  other arithmetic  45.3 us (17%)
  local copies, waits for them, and re-layouts  40.7 us (15%)
  matrix products  24.4 us (9%)
  starting transfers between devices  5.71 us (2%)
  between operations  5.46 us (2%)
    psum x5, blocking collectives, one_axis_at_a_time(): array = lax.psum(array, axis)  81.3 us
    ppermute x4, waiting for transfers between devices, passed_along(): return lax.ppermute(value, axis, pairs)  67.3 us
    gather x6, local copies, waits for them, and re-layouts, pair_measure(): phases = jnp.arctan2(jnp.diagonal(imag_part), jnp.diagonal(real_part))  27.1 us
    dot_general x3, matrix products, pair_measure(): lax.dot_general(left_side, right_side, (((1,), (1,)), ((), ())), preferre...  24.4 us
    select_n x2, other arithmetic, shards(): jnp.where(z_wrap, jnp.roll(z_later, -shifts[2], axis=-1), z_later)  15.8 us
    select_n x2, other arithmetic, shards(): jnp.where(y_wrap, jnp.roll(own_planes, -shifts[1], axis=-1), own_planes)  10.7 us
    transpose x3, local copies, waits for them, and re-layouts, pair_measure(): left_side = jnp.concatenate([own_point[0], own_point[1]], axis=1)  9 us
    reduce_sum x3, other arithmetic, pair_measure(): coherence = jnp.sum(real_part * real_part + imag_part * imag_part) / bands  7.5 us
  transfers between devices with their start and end apart: 4, of which 1 were waited for; matrix products, arithmetic and copies ran while one was open for 30% of the time, Pallas kernels for 0%

commit v1 on v0

--- a/solution.py
+++ b/solution.py
@@ -3,6 +3,7 @@
 from jax import lax
 from jax.sharding import Mesh
 from jax.sharding import PartitionSpec as P
+from jax.lax import all_gather
 
 KX = ("kx_0", "kx_1")
 KY = ("ky_0", "ky_1")
@@ -17,7 +18,7 @@
 
 def one_axis_at_a_time(array, axes):
     for axis in axes:
-        array = lax.psum(array, axis)
+        array = jnp.sum(all_gather(array, axis_name=axis), 0)
     return array
 
 

time: 271 us -> 306 us (1.13); the launches traced: 270 us -> 302 us
  blocking collectives: 81.3 us -> 113 us
    all_gather x0 -> x10, blocking collectives: none -> 113 us  [one_axis_at_a_time(): array = jnp.sum(all_gather(array, axis_name=axis), 0)]
    psum x5 -> x0, blocking collectives: 81.3 us -> none  [one_axis_at_a_time(): array = lax.psum(array, axis)]
  transfers between devices with their start and end apart: 4 -> 4, of which waited for: 1 -> 1; matrix products, arithmetic and copies ran while one was open for 30% -> 27% of each run, Pallas kernels for 0% -> 0%
where the time goes in v1:
time: 306 us; the launch traced here: 302 us
  blocking collectives  113 us (37%)
  waiting for transfers between devices  67.3 us (22%)
  other arithmetic  45.6 us (15%)
  local copies, waits for them, and re-layouts  40.8 us (13%)
  matrix products  24.4 us (8%)
  between operations  5.5 us (2%)
  starting transfers between devices  5.01 us (2%)
    all_gather x10, blocking collectives, one_axis_at_a_time(): array = jnp.sum(all_gather(array, axis_name=axis), 0)  113 us
    ppermute x4, waiting for transfers between devices, passed_along(): return lax.ppermute(value, axis, pairs)  67.3 us
    gather x6, local copies, waits for them, and re-layouts, pair_measure(): phases = jnp.arctan2(jnp.diagonal(imag_part), jnp.diagonal(real_part))  27.1 us
    dot_general x3, matrix products, pair_measure(): lax.dot_general(left_side, right_side, (((1,), (1,)), ((), ())), preferre...  24.4 us
    select_n x2, other arithmetic, shards(): jnp.where(z_wrap, jnp.roll(z_later, -shifts[2], axis=-1), z_later)  15.8 us
    select_n x2, other arithmetic, shards(): jnp.where(y_wrap, jnp.roll(own_planes, -shifts[1], axis=-1), own_planes)  10.7 us
    transpose x3, local copies, waits for them, and re-layouts, pair_measure(): left_side = jnp.concatenate([own_point[0], own_point[1]], axis=1)  9 us
    reduce_sum x3, other arithmetic, pair_measure(): coherence = jnp.sum(real_part * real_part + imag_part * imag_part) / bands  7.5 us
  transfers between devices with their start and end apart: 4, of which 1 were waited for; matrix products, arithmetic and copies ran while one was open for 27% of the time, Pallas kernels for 0%

profile of v1, /device:TPU:2, one launch (start us, length us, event | category | flops | bytes accessed | tf_op | source)
XLA Modules:
  0.0 301.5 jit_solution(8143050686592515394)
XLA Ops:
  8.2 6.5 %fusion.39 = bf16[2,1,512,2048]{3,2,1,0:T(8,128)(2,1)S(1)} fusion(bf16[2,1,512,2048]{3,2,0,1:T(8,128)(2,1)} %bitcast.103, s32[]{:T(128)S(6)} %select_n.67, pred[]{:T(512)S(6)} %eq.14), kind=kLoop, calls=%fused_computation.81 | loop fusion | flops 10485760 | bytes 8388613 | tf_op jit(solution)/shard_map/jit(_where)/select_n | solution.py:59
  18.3 4.2 %fusion.24 = bf16[2,1,512,2048]{3,2,0,1:T(8,128)(2,1)S(1)} fusion(bf16[2,1,512,2048]{3,2,0,1:T(8,128)(2,1)S(1)} %bitcast.104, s32[]{:T(128)S(6)} %select_n.67, pred[]{:T(512)S(6)} %eq.14), kind=kLoop, calls=%fused_computation.39 | loop fusion | flops 10485760 | bytes 8388613 | tf_op jit(solution)/shard_map/jit(_where)/select_n | solution.py:59
  26.5 67.3 %collective-permute-done.2 = bf16[2,1,512,2048]{3,2,0,1:T(8,128)(2,1)} collective-permute-done((bf16[2,1,512,2048]{3,2,0,1:T(8,128)(2,1)}, bf16[2,1,512,2048]{3,2,0,1:T(8,128)(2,1)}, u32[]{:S(2)}, u32[]{:S(2)}) %collective-permute-start.2) | collective-permute-done | bytes 4194336 | tf_op jit(solution)/shard_map/ppermute | solution.py:16
  93.9 7.8 %fusion.40 = bf16[2,1,512,2048]{3,2,1,0:T(8,128)(2,1)S(1)} fusion(bf16[2,1,512,2048]{3,2,0,1:T(8,128)(2,1)} %collective-permute-done.2, s32[]{:T(128)S(6)} %select_n.69, pred[]{:T(512)S(6)} %eq.15), kind=kLoop, calls=%fused_computation.82 | loop fusion | flops 10485760 | bytes 8388613 | tf_op jit(solution)/shard_map/jit(_where)/select_n | solution.py:64
  102.0 8.0 %fusion.22 = bf16[2,1,512,2048]{3,2,0,1:T(8,128)(2,1)S(1)} fusion(bf16[2,1,512,2048]{3,2,0,1:T(8,128)(2,1)} %collective-permute-done.2, s32[]{:T(128)S(6)} %select_n.69, pred[]{:T(512)S(6)} %eq.15), kind=kLoop, calls=%fused_computation.37 | loop fusion | flops 10485760 | bytes 8388613 | tf_op jit(solution)/shard_map/jit(_where)/select_n | solution.py:64
  110.1 8.2 %fusion.29 = f32[1,512,1024]{2,1,0:T(8,128)} fusion(bf16[1,512,2048]{2,1,0:T(8,128)(2,1)S(1)} %fusion.36, bf16[1,512,2048]{2,1,0:T(8,128)(2,1)S(1)} %slice_bitcast_fusion, bf16[1,512,2048]{2,1,0:T(8,128)(2,1)S(1)} %slice_bitcast_fusion.1, bf16[1,512,2048]{2,1,0:T(8,128)(2,1)} %get-tuple-element.8, bf16[1,512,2048]{2,1,0:T(8,128)(2,1)} %get-tuple-element.7), kind=kOutput, calls=%fused_computation.54 | convolution fusion | flops 4336910336 | bytes 12582912 | tf_op jit(solution)/shard_map/vmap()/dot_general | solution.py:35
  120.8 4.5 %gather_fusion.4 = f32[512]{0:T(512)S(1)} fusion(f32[512,512]{1,0:T(8,128)S(1)} %get-tuple-element.17, s32[512]{0:T(512)S(1)} %bitcast.94), kind=kCustom, calls=%fused_computation.4 | custom fusion | bytes 8192 | tf_op jit(solution)/shard_map/vmap(jit(diagonal))/cond/branch_0_fun/gather | solution.py:40
  125.3 4.5 %gather_fusion.5 = f32[512]{0:T(512)S(1)} fusion(f32[512,512]{1,0:T(8,128)S(1)} %get-tuple-element.16, s32[512]{0:T(512)S(1)} %bitcast.95), kind=kCustom, calls=%fused_computation.5 | custom fusion | bytes 8192 | tf_op jit(solution)/shard_map/vmap(jit(diagonal))/cond/branch_0_fun/gather | solution.py:40
  129.9 3.3 %slice_bitcast_fusion.5 = bf16[1,512,2048]{2,1,0:T(8,128)(2,1)} fusion(bf16[2,1,512,2048]{3,2,1,0:T(8,128)(2,1)} %bitcast.12), kind=kLoop, calls=%fused_computation.51 | loop fusion | bytes 4194304 | tf_op jit(solution)/shard_map/vmap()/squeeze;vmap()/transpose | solution.py:27
  136.4 8.1 %fusion.30 = f32[1,512,1024]{2,1,0:T(8,128)} fusion(bf16[1,512,2048]{2,1,0:T(8,128)(2,1)S(1)} %copy-done.1, bf16[1,512,2048]{2,1,0:T(8,128)(2,1)S(1)} %copy-done.3, bf16[1,512,2048]{2,1,0:T(8,128)(2,1)S(1)} %copy-done.2, bf16[1,512,2048]{2,1,0:T(8,128)(2,1)} %slice_bitcast_fusion.4, bf16[1,512,2048]{2,1,0:T(8,128)(2,1)} %slice_bitcast_fusion.5), kind=kOutput, calls=%fused_computation.55 | convolution fusion | flops 4336910336 | bytes 12582912 | tf_op jit(solution)/shard_map/vmap()/dot_general | solution.py:35
  147.0 4.5 %gather_fusion.2 = f32[512]{0:T(512)S(1)} fusion(f32[512,512]{1,0:T(8,128)S(1)} %get-tuple-element.14, s32[512]{0:T(512)S(1)} %bitcast.96), kind=kCustom, calls=%fused_computation.2 | custom fusion | bytes 8192 | tf_op jit(solution)/shard_map/vmap(jit(diagonal))/cond/branch_0_fun/gather | solution.py:40
  151.5 4.5 %gather_fusion.3 = f32[512]{0:T(512)S(1)} fusion(f32[512,512]{1,0:T(8,128)S(1)} %get-tuple-element.13, s32[512]{0:T(512)S(1)} %bitcast.97), kind=kCustom, calls=%fused_computation.3 | custom fusion | bytes 8192 | tf_op jit(solution)/shard_map/vmap(jit(diagonal))/cond/branch_0_fun/gather | solution.py:40
  156.1 6.7 %fusion.26 = bf16[2,512,2048]{2,1,0:T(8,128)(2,1)S(1)} fusion(bf16[2,512,2048]{2,1,0:T(8,128)(2,1)} %collective-permute-done, s32[]{:T(128)S(6)} %select_n.58, pred[]{:T(512)S(6)} %eq.13), kind=kLoop, calls=%fused_computation.41 | loop fusion | flops 10485760 | bytes 8388613 | tf_op jit(solution)/shard_map/jit(_where)/select_n | solution.py:54
  163.2 8.1 %fusion.31 = f32[1,512,1024]{2,1,0:T(8,128)} fusion(bf16[1,512,2048]{2,1,0:T(8,128)(2,1)S(1)} %get-tuple-element.5, bf16[1,512,2048]{2,1,0:T(8,128)(2,1)S(1)} %get-tuple-element.6, bf16[1,512,2048]{2,1,0:T(8,128)(2,1)S(1)} %get-tuple-element.4, bf16[1,512,2048]{2,1,0:T(8,128)(2,1)} %get-tuple-element.8, bf16[1,512,2048]{2,1,0:T(8,128)(2,1)} %get-tuple-element.7), kind=kOutput, calls=%fused_computation.56 | convolution fusion | flops 4336910336 | bytes 12582912 | tf_op jit(solution)/shard_map/vmap()/dot_general | solution.py:35
  173.8 4.5 %gather_fusion = f32[512]{0:T(512)S(1)} fusion(f32[512,512]{1,0:T(8,128)S(1)} %get-tuple-element.11, s32[512]{0:T(512)S(1)} %bitcast.98), kind=kCustom, calls=%fused_computation | custom fusion | bytes 8192 | tf_op jit(solution)/shard_map/vmap(jit(diagonal))/cond/branch_0_fun/gather | solution.py:40
  178.4 4.5 %gather_fusion.1 = f32[512]{0:T(512)S(1)} fusion(f32[512,512]{1,0:T(8,128)S(1)} %get-tuple-element.10, s32[512]{0:T(512)S(1)} %bitcast.99), kind=kCustom, calls=%fused_computation.1 | custom fusion | bytes 8192 | tf_op jit(solution)/shard_map/vmap(jit(diagonal))/cond/branch_0_fun/gather | solution.py:40
  183.0 28.5 %all-gather = f32[24,1,512]{2,1,0:T(1,128)S(1)} all-gather(f32[3,1,512]{2,1,0:T(1,128)S(1)} %pad_maximum_fusion), channel_id=2, replica_groups=mesh['kx_0'=8,'kx_1'=2,'ky_0'=2,'ky_1'=2,'kz'=4] {'kx_0'}, dimensions={0}, use_global_device_ids=true | all-gather | bytes 55296 | tf_op jit(solution)/shard_map/all_gather | solution.py:21
  211.7 16.3 %all-gather.9 = f32[2,3,512]{2,1,0:T(4,128)S(1)} all-gather(f32[1,3,512]{2,1,0:T(4,128)S(1)} %bitcast.105), channel_id=3, replica_groups=mesh['kx_0'=8,'kx_1'=2,'ky_0'=2,'ky_1'=2,'kz'=4] {'kx_1'}, dimensions={0}, use_global_device_ids=true | all-gather | bytes 18432 | tf_op jit(solution)/shard_map/all_gather | solution.py:21
  228.0 5.9 %all-gather.10 = f32[2,3,512]{2,1,0:T(4,128)S(1)} all-gather(f32[1,3,512]{2,1,0:T(4,128)S(1)} %bitcast.106), channel_id=4, replica_groups=mesh['kx_0'=8,'kx_1'=2,'ky_0'=2,'ky_1'=2,'kz'=4] {'ky_0'}, dimensions={0}, use_global_device_ids=true | all-gather | bytes 18432 | tf_op jit(solution)/shard_map/all_gather | solution.py:21
  235.7 11.9 %all-gather.12 = f32[4,3,512]{2,1,0:T(4,128)S(1)} all-gather(f32[1,3,512]{2,1,0:T(4,128)S(1)} %bitcast.108), channel_id=6, replica_groups=mesh['kx_0'=8,'kx_1'=2,'ky_0'=2,'ky_1'=2,'kz'=4] {'kz'}, dimensions={0}, use_global_device_ids=true | all-gather | bytes 30720 | tf_op jit(solution)/shard_map/all_gather | solution.py:21
  247.7 24.6 %all_gather.68 = f32[8,3,512]{2,1,0:T(4,128)S(1)} all-gather(f32[1,3,512]{2,1,0:T(4,128)S(1)} %maximum_multiply_fusion), channel_id=1, replica_groups=mesh['kx_0'=8,'kx_1'=2,'ky_0'=2,'ky_1'=2,'kz'=4] {'kx_0'}, dimensions={0}, use_global_device_ids=true | all-gather | bytes 55296 | tf_op jit(solution)/shard_map/all_gather | solution.py:21
  272.3 4.4 %all-gather.13 = f32[2,3,512]{2,1,0:T(4,128)S(1)} all-gather(f32[1,3,512]{2,1,0:T(4,128)S(1)} %bitcast.109), channel_id=7, replica_groups=mesh['kx_0'=8,'kx_1'=2,'ky_0'=2,'ky_1'=2,'kz'=4] {'kx_1'}, dimensions={0}, use_global_device_ids=true | all-gather | bytes 18432 | tf_op jit(solution)/shard_map/all_gather | solution.py:21
  276.7 5.9 %all-gather.14 = f32[2,3,512]{2,1,0:T(4,128)S(1)} all-gather(f32[1,3,512]{2,1,0:T(4,128)S(1)} %bitcast.110), channel_id=8, replica_groups=mesh['kx_0'=8,'kx_1'=2,'ky_0'=2,'ky_1'=2,'kz'=4] {'ky_0'}, dimensions={0}, use_global_device_ids=true | all-gather | bytes 18432 | tf_op jit(solution)/shard_map/all_gather | solution.py:21
  284.4 11.9 %all-gather.16 = f32[4,3,512]{2,1,0:T(4,128)S(1)} all-gather(f32[1,3,512]{2,1,0:T(4,128)S(1)} %bitcast.112), channel_id=10, replica_groups=mesh['kx_0'=8,'kx_1'=2,'ky_0'=2,'ky_1'=2,'kz'=4] {'kz'}, dimensions={0}, use_global_device_ids=true | all-gather | bytes 30720 | tf_op jit(solution)/shard_map/all_gather | solution.py:21
  (55 shorter events, 31.3 us)
Async XLA Ops:
  0.6 93.2 %collective-permute-start.2 = (bf16[2,1,512,2048]{3,2,0,1:T(8,128)(2,1)}, bf16[2,1,512,2048]{3,2,0,1:T(8,128)(2,1)}, u32[]{:S(2)}, u32[]{:S(2)}) collective-permute-start(bf16[2,1,512,2048]{3,2,0,1:T(8,128)(2,1)} %bitcast.100), channel_id=1, source_target_pairs={{0,3},{1,0},{2,1},{3,2},{4,7},{5,4},{6,5},{7,6},{8,11},{9,8},{10,9... | collective-permute-start | bytes 12582920 | tf_op jit(solution)/shard_map/ppermute | solution.py:16
  3.7 126.1 %collective-permute-start.1 = (bf16[2,1,512,2048]{3,2,0,1:T(8,128)(2,1)}, bf16[2,1,512,2048]{3,2,0,1:T(8,128)(2,1)}, u32[]{:S(2)}, u32[]{:S(2)}) collective-permute-start(bf16[2,1,512,2048]{3,2,0,1:T(8,128)(2,1)} %bitcast.101), channel_id=1, source_target_pairs={{0,4},{4,8},{8,12},{12,0},{1,5},{5,9},{9,13},{13,1},{2,6},{6,10},{... | collective-permute-start | bytes 12582920 | tf_op jit(solution)/shard_map/ppermute | solution.py:16
  3.7 152.3 %collective-permute-start = (bf16[2,512,2048]{2,1,0:T(8,128)(2,1)}, bf16[2,512,2048]{2,1,0:T(8,128)(2,1)}, u32[]{:S(2)}, u32[]{:S(2)}) collective-permute-start(bf16[2,512,2048]{2,1,0:T(8,128)(2,1)} %bitcast.102), channel_id=1, source_target_pairs={{0,240},{16,0},{32,16},{48,32},{64,48},{80,64},{96,80},{112,96},{1... | collective-permute-start | bytes 12582920 | tf_op jit(solution)/shard_map/ppermute | solution.py:16
  14.7 3.6 %copy-start = (bf16[2,1,1,1,512,2048]{5,4,3,2,1,0:T(8,128)(2,1)S(1)}, bf16[2,1,1,1,512,2048]{5,4,3,2,1,0:T(8,128)(2,1)}, u32[]{:S(2)}) copy-start(bf16[2,1,1,1,512,2048]{5,4,3,2,1,0:T(8,128)(2,1)} %param.5) | copy-start | bytes 12582916
  129.9 6.6 %copy-start.1 = (bf16[1,512,2048]{2,1,0:T(8,128)(2,1)S(1)}, bf16[1,512,2048]{2,1,0:T(8,128)(2,1)}, u32[]{:S(2)}) copy-start(bf16[1,512,2048]{2,1,0:T(8,128)(2,1)} %fusion.35) | copy-start | bytes 6291460
  129.9 6.5 %copy-start.2 = (bf16[1,512,2048]{2,1,0:T(8,128)(2,1)S(1)}, bf16[1,512,2048]{2,1,0:T(8,128)(2,1)}, u32[]{:S(2)}) copy-start(bf16[1,512,2048]{2,1,0:T(8,128)(2,1)} %slice_bitcast_fusion.3) | copy-start | bytes 6291460
  129.9 6.5 %copy-start.3 = (bf16[1,512,2048]{2,1,0:T(8,128)(2,1)S(1)}, bf16[1,512,2048]{2,1,0:T(8,128)(2,1)}, u32[]{:S(2)}) copy-start(bf16[1,512,2048]{2,1,0:T(8,128)(2,1)} %slice_bitcast_fusion.2) | copy-start | bytes 6291460
  171.3 128.3 %copy-start.4 = (f32[3]{0:T(128)S(1)}, f32[3]{0:T(128)}, u32[]{:S(2)}) copy-start(f32[3]{0:T(128)} %constant.109) | copy-start | bytes 40
  171.3 128.4 %copy-start.5 = (f32[3]{0:T(128)S(1)}, f32[3]{0:T(128)}, u32[]{:S(2)}) copy-start(f32[3]{0:T(128)} %constant.106) | copy-start | bytes 40
  297.6 2.7 collective-permute-start.3
